TPU v7x, 32 devices: a whole 2x2x4 slice. The times are simulated.
32 devices in a mesh: wide: 16 (over z, y, x), tall: 2 (over core).
Axes of the slice: x: 2, y: 2, z: 4, core: 2. Of those that a mesh axis runs over, the one named last changes fastest.
Arguments:
- tokens: bfloat16 [48, 384, 512], P('tall', 'wide'), may hold values from -6 to 6
- qkv_weight: bfloat16 [512, 1536], replicated, may hold values from -0.25 to 0.25
- proj_weight: bfloat16 [512, 512], replicated, may hold values from -0.25 to 0.25
- head_scale: float32 [16], replicated, may hold values from 5 to 100
- attn_gain: float32 [512], replicated, may hold values from 0.5 to 1.5
- router: bfloat16 [512, 16], replicated, may hold values from -0.25 to 0.25
- expert_in: bfloat16 [16, 512, 2048], P('wide', None, 'tall'), may hold values from -0.25 to 0.25
- expert_out: bfloat16 [16, 2048, 512], P('wide', 'tall'), may hold values from -0.125 to 0.125
- moe_gain: float32 [512], replicated, may hold values from 0.5 to 1.5
- expert_ids: int32 [2, 16, 576, 1], P('tall', 'wide'), may hold values from 0 to 15; in each aligned block of 576 rows (0 to 575, 576 to 1151, ..., all dimensions but the last counted through in order) at most 54 rows name the same one
- keep: int32 [2, 16, 576], P('tall', 'wide'), may hold values 0 or 1
Outputs:
- mixed: bfloat16 [48, 384, 512], P('tall', 'wide')
Inputs may be any that keep to these rules, and one draw needn't show every extreme that they name: `expert_ids`: within the tokens of one tile (one index of the first two dimensions), no expert is named more than 54 times, a bound that some block reaches.
All inputs are finite; a program needn't handle non-finite values. No bound on the sum of `keep` on one device may be relied on, other than what follows from the above.
Results may differ from a plain program's by a relative error of at most 0.012.
The roundings to bfloat16 on the way count: a program that leaves them out, or rounds other values in their place, can miss the bound.
Values may be sent and summed in bfloat16 or wider, within the bound.
No kernel may reach another device: no remote copies, remote signals or barrier semaphores. Data moves between devices by JAX's collectives and lax.ppermute only.
A program may use at most 64 MiB of HBM per device.

v0:
```python
import functools

import jax
import jax.numpy as jnp
from jax import lax
from jax.experimental import pallas as pl
from jax.experimental.pallas import tpu as pltpu
from jax.sharding import PartitionSpec as P

LANES = 128
VM = pl.BlockSpec(memory_space=pltpu.VMEM)
SM = pl.BlockSpec(memory_space=pltpu.SMEM)
HB = pl.BlockSpec(memory_space=pltpu.HBM)
LOG2E = 1.4426950408889634


CHUNKS = 1


def chunk_sizes(room):
    tiles = room // 8
    count = min(CHUNKS, tiles)
    return [8 * (tiles * (i + 1) // count - tiles * i // count) for i in range(count)]


def shifted(value, axis, by):
    peers = lax.axis_size(axis)
    return lax.ppermute(value, axis, [(i, (i + by) % peers) for i in range(peers)])


def dot(a, b):
    return jnp.dot(a, b, preferred_element_type=jnp.float32)


def attn_kernel(
    grid_rc,
    head_dim,
    edge,
    rows_q,
    stop,
    unroll,
    first_ref,
    scale_ref,
    win_ref,
    wqkv_ref,
    wproj_ref,
    gain_ref,
    target_ref,
    x1_ref,
    *rest_refs,
):
    *sent_refs, q_s, att_s, kbig_s, vbig_s, sa_s, sb_s, out_s, sem = rest_refs
    total_rows, total_cols, shift = grid_rc
    count, feature = win_ref.shape
    groups = feature // LANES
    heads = LANES // head_dim
    main = count // LANES * LANES
    rest = count - main
    regions, terms = 4, 3
    feats = regions * terms
    win = win_ref[...]

    flat = lax.broadcasted_iota(jnp.int32, (count, LANES), 0)
    lane = lax.broadcasted_iota(jnp.int32, (count, LANES), 1)
    low = (first_ref[0] + flat // edge + shift >= total_rows).astype(jnp.int32)
    right = (first_ref[1] + flat % edge + shift >= total_cols).astype(jnp.int32)
    used = lane < heads * feats
    same = (2 * low + right) == (lane % feats) // terms
    kfeat = jnp.where(used & jnp.logical_not(same), 1.0, 0.0).astype(jnp.bfloat16)
    qmatch = used & same

    wide = 2 * LANES
    r_i = lax.broadcasted_iota(jnp.int32, (wide, wide), 0) // head_dim
    c_i = lax.broadcasted_iota(jnp.int32, (wide, wide), 1) // head_dim
    block = jnp.where(r_i == c_i, 1.0, 0.0).astype(jnp.bfloat16)

    def unit(value):
        sq = value * value
        hi = sq.astype(jnp.bfloat16)
        lo = (sq - hi.astype(jnp.float32)).astype(jnp.bfloat16)
        total = dot(hi, block) + dot(lo, block)
        return (value * lax.rsqrt(total + 1e-06)).astype(jnp.bfloat16)

    head_of = lane // head_dim
    krow = lax.broadcasted_iota(jnp.int32, (wide, LANES), 0)
    khead = jnp.where(krow < LANES, krow // head_dim, (krow - LANES) // feats)
    klane = lax.broadcasted_iota(jnp.int32, (wide, LANES), 1)
    lane1 = lax.broadcasted_iota(jnp.int32, (8, LANES), 1)
    lane_head = lane1 // feats
    lane_term = lane1 % terms
    zero = jnp.zeros((), jnp.bfloat16)
    per_tile = LANES // rest if rest else 1
    kfeat_t = kfeat.T
    ones = [jnp.where(head_of == h, 1.0, 0.0).astype(jnp.bfloat16) for h in range(heads)]

    def place(g, q, k, v):
        kt = jnp.concatenate([k.T, kfeat_t], axis=0)
        for h in range(heads):
            for t in range(main // LANES):
                kbig_s[g, :, h * main + t * LANES : h * main + (t + 1) * LANES] = jnp.where(
                    khead == h, kt[:, t * LANES : (t + 1) * LANES], zero
                )
            vm = jnp.concatenate([jnp.where(head_of == h, v, zero), ones[h]], axis=1)
            vbig_s[g, h * main : (h + 1) * main, :] = vm[:main]
            if rest:
                vbig_s[g, heads * main + h * rest : heads * main + (h + 1) * rest, :] = vm[main:]
        if rest:
            tail = jnp.concatenate([kt[:, main:]] * per_tile, axis=1)
            for t in range(heads // per_tile):
                kbig_s[g, :, heads * main + t * LANES : heads * main + (t + 1) * LANES] = jnp.where(
                    khead == t * per_tile + klane // rest, tail, zero
                )
        scale = jnp.full((8, LANES), scale_ref[g * heads], jnp.float32)
        for h in range(1, heads):
            scale = jnp.where(lane_head == h, scale_ref[g * heads + h], scale)
        off = -100.0 / scale
        b0 = off.astype(jnp.bfloat16).astype(jnp.float32)
        b1 = (off - b0).astype(jnp.bfloat16).astype(jnp.float32)
        b2 = off - b0 - b1
        piece = jnp.where(lane_term == 0, b0, jnp.where(lane_term == 1, b1, b2))[:1]
        q_s[g, :, :LANES] = q
        q_s[g, :, LANES:] = jnp.where(qmatch, piece, 0.0).astype(jnp.bfloat16)

    for p in range(feature // wide):
        at = p * wide
        qn = unit(dot(win, wqkv_ref[:, at : at + wide]))
        kn = unit(dot(win, wqkv_ref[:, feature + at : feature + at + wide]))
        vb = dot(win, wqkv_ref[:, 2 * feature + at : 2 * feature + at + wide]).astype(jnp.bfloat16)
        for half in range(2):
            part = slice(half * LANES, (half + 1) * LANES)
            place(2 * p + half, qn[:, part], kn[:, part], vb[:, part])
    if stop < 1:
        x1_ref[...] = win
        return

    tail_lane = lax.broadcasted_iota(jnp.int32, (rows_q, LANES), 1)

    def scores(g, b):
        return dot(q_s[g, pl.ds(b * rows_q, rows_q), :], kbig_s[g])

    def finish(g, b, s_ref):
        factors = [scale_ref[g * heads + h] * LOG2E for h in range(heads)]
        tops, es = [], []
        for h in range(heads):
            tiles = [s_ref[:, h * main + t * LANES : h * main + (t + 1) * LANES] for t in range(main // LANES)]
            if rest:
                t = h // per_tile
                tile = s_ref[:, heads * main + t * LANES : heads * main + (t + 1) * LANES]
                tiles.append(jnp.where(tail_lane // rest == h % per_tile, tile, -3e38))
            top = functools.reduce(jnp.maximum, tiles)
            tops.append(jnp.max(top, axis=1, keepdims=True))
        for h in range(heads):
            e = jnp.exp2((s_ref[:, h * main : (h + 1) * main] - tops[h]) * factors[h])
            es.append(e.astype(jnp.bfloat16))
        if rest:
            for t in range(heads // per_tile):
                top = jnp.broadcast_to(tops[t * per_tile], (rows_q, LANES))
                factor = jnp.full((rows_q, LANES), factors[t * per_tile], jnp.float32)
                for j in range(1, per_tile):
                    top = jnp.where(tail_lane // rest == j, tops[t * per_tile + j], top)
                    factor = jnp.where(tail_lane // rest == j, factors[t * per_tile + j], factor)
                tile = s_ref[:, heads * main + t * LANES : heads * main + (t + 1) * LANES]
                es.append(jnp.exp2((tile - top) * factor).astype(jnp.bfloat16))
        o = dot(jnp.concatenate(es, axis=1), vbig_s[g])
        col = g * LANES if isinstance(g, int) else pl.multiple_of(g * LANES, LANES)
        att_s[b * rows_q : (b + 1) * rows_q, pl.ds(col, LANES)] = (o[:, :LANES] / o[:, LANES:]).astype(jnp.bfloat16)

    blocks = count // rows_q
    bufs = [sa_s, sb_s]
    sa_s[...] = scores(0, 0)
    if unroll:
        work = [(g, b) for g in range(groups) for b in range(blocks)]
        for i, (g, b) in enumerate(work):
            if i + 1 < len(work):
                bufs[(i + 1) % 2][...] = scores(*work[i + 1])
            finish(g, b, bufs[i % 2])
    else:
        def step(g, carry):
            for b in range(blocks):
                nxt = (g, b + 1) if b + 1 < blocks else (jnp.minimum(g + 1, groups - 1), 0)
                bufs[(b + 1) % 2][...] = scores(*nxt)
                finish(g, b, bufs[b % 2])
            return carry

        lax.fori_loop(0, groups, step, 0)
    if stop < 2:
        x1_ref[...] = att_s[...]
        return

    out = dot(att_s[...], wproj_ref[...])
    mean = jnp.mean(out, axis=1, keepdims=True)
    cent = out - mean
    var = jnp.mean(cent * cent, axis=1, keepdims=True)
    x1 = (win.astype(jnp.float32) + cent * lax.rsqrt(var + 1e-05) * gain_ref[...]).astype(jnp.bfloat16)
    x1_ref[...] = x1

    if stop < 3:
        return
    target = target_ref[...]
    copies, base = [], 0
    for i, sent_ref in enumerate(sent_refs):
        rows = sent_ref.shape[0]
        slot = base + lax.broadcasted_iota(jnp.int32, (rows, count), 0)
        pick = jnp.where(slot == target, 1.0, 0.0).astype(jnp.bfloat16)
        out_s[base : base + rows, :] = dot(pick, x1).astype(jnp.bfloat16)
        copies.append(pltpu.make_async_copy(out_s.at[pl.ds(base, rows)], sent_ref, sem.at[i]))
        copies[-1].start()
        base += rows
    for copy in copies:
        copy.wait()


def call_attn(first, head_scale, rolled, qkv, proj, gain, target, *, grid_rc, edge, sizes, rows_q=None, stop=9, unroll=1):
    count, feature = rolled.shape
    rows_q = rows_q or count // 2
    head_dim = feature // head_scale.shape[0]
    groups = feature // LANES
    return pl.pallas_call(
        functools.partial(attn_kernel, grid_rc, head_dim, edge, rows_q, stop, unroll),
        out_shape=(
            jax.ShapeDtypeStruct((count, feature), jnp.bfloat16),
            *[pltpu.HBM((rows, feature), jnp.bfloat16) for rows in sizes],
        ),
        in_specs=[SM, SM, VM, VM, VM, VM, VM],
        out_specs=(VM, *[HB] * len(sizes)),
        scratch_shapes=[
            pltpu.VMEM((groups, count, 2 * LANES), jnp.bfloat16),
            pltpu.VMEM((count, feature), jnp.bfloat16),
            pltpu.VMEM((groups, 2 * LANES, LANES // head_dim * count), jnp.bfloat16),
            pltpu.VMEM((groups, LANES // head_dim * count, 2 * LANES), jnp.bfloat16),
            pltpu.VMEM((rows_q, LANES // head_dim * count), jnp.float32),
            pltpu.VMEM((rows_q, LANES // head_dim * count), jnp.float32),
            pltpu.VMEM((sum(sizes), feature), jnp.bfloat16),
            pltpu.SemaphoreType.DMA((len(sizes),)),
        ],
        compiler_params=pltpu.CompilerParams(vmem_limit_bytes=32 * 1024 * 1024),
        name="attention",
    )(first, head_scale, rolled, qkv, proj, gain, target)


def expert_kernel(parts, row_block, x_ref, *refs):
    w_in, w_out, y_ref = refs[:parts], refs[parts : 2 * parts], refs[2 * parts]
    in_s, out_s, acc_s, sem = refs[2 * parts + 1 :]
    rows = x_ref.shape[0]
    copies = []
    for n in range(parts):
        copies.append(pltpu.make_async_copy(w_in[n], in_s.at[n], sem.at[2 * n]))
        copies.append(pltpu.make_async_copy(w_out[n], out_s.at[n], sem.at[2 * n + 1]))
    for copy in copies:
        copy.start()
    for n in range(parts):
        copies[2 * n].wait()
        copies[2 * n + 1].wait()
        for i in range(rows // row_block):
            part = slice(i * row_block, (i + 1) * row_block)
            h = dot(x_ref[part, :], in_s[n])
            h = (0.5 * h * (1.0 + lax.erf(h * 0.7071067811865476))).astype(jnp.bfloat16)
            y = dot(h, out_s[n])
            if n:
                y = acc_s[part, :] + y
            if n < parts - 1:
                acc_s[part, :] = y
            else:
                y_ref[part, :] = y.astype(jnp.bfloat16)


def gate_kernel(x1_ref, router_ref, target_ref, ids_ref, pick_ref, scaled_ref):
    count, slots = pick_ref.shape
    target = target_ref[...]
    slot = lax.broadcasted_iota(jnp.int32, (count, slots), 1)
    pick_ref[...] = jnp.where(slot == target, 1.0, 0.0).astype(jnp.bfloat16)
    logits = dot(x1_ref[...], router_ref[...])
    mine = lax.broadcasted_iota(jnp.int32, logits.shape, 1) == ids_ref[...]
    logit = jnp.sum(jnp.where(mine, logits, 0.0), axis=1, keepdims=True)
    scaled_ref[...] = jnp.where(target < slots, jax.nn.sigmoid(logit), 0.0)


def combine_kernel(row_block, x1_ref, pick_ref, scaled_ref, gain_ref, *refs):
    *back_refs, out_ref = refs
    for i in range(x1_ref.shape[0] // row_block):
        at = slice(i * row_block, (i + 1) * row_block)
        y, base = None, 0
        for back_ref in back_refs:
            rows = back_ref.shape[0]
            term = dot(pick_ref[at, base : base + rows], back_ref[...])
            y = term if y is None else y + term
            base += rows
        mean = jnp.mean(y, axis=1, keepdims=True)
        cent = y - mean
        var = jnp.mean(cent * cent, axis=1, keepdims=True)
        add = scaled_ref[at, :] * (cent * lax.rsqrt(var + 1e-05) * gain_ref[...])
        out_ref[at, :] = (x1_ref[at, :].astype(jnp.float32) + add).astype(jnp.bfloat16)


def params(mib):
    return pltpu.CompilerParams(vmem_limit_bytes=mib * 1024 * 1024)


def body(
    tokens,
    qkv_weight,
    proj_weight,
    head_scale,
    attn_gain,
    router,
    expert_in,
    expert_out,
    moe_gain,
    expert_ids,
    keep,
):
    tile_rows, edge, feature = tokens.shape
    shift = edge // 2
    tall = lax.axis_size("tall")
    count = tile_rows * edge

    column_part = shifted(tokens[:, :shift], "wide", -1)
    widened = jnp.concatenate([tokens[:, shift:], column_part], axis=1)
    row_part = shifted(widened[:shift], "tall", -1)
    rolled = jnp.concatenate([widened[shift:], row_part], axis=0).reshape(count, feature)

    w_in = [expert_in[0]] + [shifted(expert_in[0], "tall", -n) for n in range(1, tall)]
    w_out = [expert_out[0]] + [shifted(expert_out[0], "tall", -n) for n in range(1, tall)]

    total_rows = tile_rows * tall
    total_cols = edge * lax.axis_size("wide")
    first = jnp.stack([lax.axis_index("tall") * tile_rows, lax.axis_index("wide") * edge]).astype(jnp.int32)

    route_ids = expert_ids[0, 0, :, 0]
    keep_flag = keep[0, 0]
    experts = router.shape[1]
    capacity = max(2, 3 * count // (2 * experts))
    room = -(-capacity // 8) * 8
    onehot = (route_ids[:, None] == jnp.arange(experts, dtype=jnp.int32)[None, :]).astype(jnp.int32)
    live_hits = onehot * keep_flag[:, None]
    before = jnp.cumsum(live_hits, axis=0) - live_hits
    slot_ids = jnp.sum(before * onehot, axis=1)
    parts = chunk_sizes(room)
    slots = experts * room
    row, start = jnp.zeros_like(slot_ids), 0
    for part in parts:
        here = experts * start + route_ids * part + slot_ids - start
        row = jnp.where((slot_ids >= start) & (slot_ids < start + part), here, row)
        start += part
    target = jnp.where(keep_flag == 1, row, slots)

    x1, *sent = call_attn(
        first,
        head_scale,
        rolled,
        qkv_weight,
        proj_weight,
        attn_gain[None, :],
        target[None, :],
        grid_rc=(total_rows, total_cols, shift),
        edge=edge,
        sizes=tuple(experts * part for part in parts),
    )
    hidden = w_in[0].shape[1]
    weights = [pltpu.with_memory_space_constraint(w, pltpu.HBM) for w in w_in + w_out]

    def exchange(value):
        rows = value.shape[0]
        value = value.reshape(experts, rows // experts, feature)
        return lax.all_to_all(value, "wide", split_axis=0, concat_axis=0, tiled=True).reshape(rows, feature)

    def run_experts(value):
        rows = value.shape[0]
        return pl.pallas_call(
            functools.partial(expert_kernel, tall, rows // 2 if rows > 512 else rows),
            out_shape=pltpu.HBM((rows, feature), jnp.bfloat16),
            in_specs=[VM] + [HB] * (2 * tall),
            out_specs=VM,
            scratch_shapes=[
                pltpu.VMEM((tall, feature, hidden), jnp.bfloat16),
                pltpu.VMEM((tall, hidden, feature), jnp.bfloat16),
                pltpu.VMEM((rows, feature), jnp.float32),
                pltpu.SemaphoreType.DMA((2 * tall,)),
            ],
            compiler_params=params(32),
            cost_estimate=pl.CostEstimate(
                flops=4 * rows * feature * hidden * tall, bytes_accessed=4 * feature * hidden * tall, transcendentals=0
            ),
        )(value, *weights)

    arrived = []
    for value in sent:
        arrived.append(exchange(value))
    returned = []
    for value in arrived:
        made = run_experts(value)
        returned.append(exchange(made))

    pick, scaled = pl.pallas_call(
        gate_kernel,
        out_shape=(
            jax.ShapeDtypeStruct((count, slots), jnp.bfloat16),
            jax.ShapeDtypeStruct((count, 1), jnp.float32),
        ),
        in_specs=[VM] * 4,
        out_specs=(VM, VM),
        compiler_params=params(16),
        name="gate",
    )(x1, router, target[:, None], route_ids[:, None])
    result = pl.pallas_call(
        functools.partial(combine_kernel, count // 2),
        out_shape=jax.ShapeDtypeStruct((count, feature), jnp.bfloat16),
        in_specs=[VM] * (4 + len(parts)),
        out_specs=VM,
        compiler_params=params(16),
        name="combine",
    )(x1, pick, scaled, moe_gain[None, :], *returned)
    return result.reshape(tile_rows, edge, feature)


def solution(mesh):
    placed = (
        P("tall", "wide", None),
        P(),
        P(),
        P(),
        P(),
        P(),
        P("wide", None, "tall"),
        P("wide", "tall", None),
        P(),
        P("tall", "wide", None, None),
        P("tall", "wide", None),
    )
    return jax.shard_map(
        body, mesh=mesh, in_specs=placed, out_specs=P("tall", "wide", None), check_vma=False
    )
```

profile of v0, /device:TPU:0, one launch (start us, length us, event | category | flops | bytes accessed | tf_op | source)
XLA Modules:
  0.0 95.7 jit_solution(9221058553069151260)
XLA Ops:
  0.0 1.3 %fusion.7 = (bf16[24,12,512]{2,1,0:T(8,128)(2,1)S(1)}, bf16[24,12,512]{2,1,0:T(8,128)(2,1)S(1)}) fusion(bf16[24,24,512]{2,1,0:T(8,128)(2,1)} %param.11), kind=kLoop, calls=%fused_computation.27 | loop fusion | bytes 1179648 | tf_op jit(solution)/shard_map/slice | solution.py:318
  1.3 0.0 copy-start
  1.3 0.0 copy-start.1
  1.3 0.0 copy-start.3
  1.3 7.0 %collective-permute-start = (bf16[24,12,512]{2,1,0:T(8,128)(2,1)S(1)}, bf16[24,12,512]{2,1,0:T(8,128)(2,1)S(1)}, u32[]{:S(2)}, u32[]{:S(2)}) collective-permute-start(bf16[24,12,512]{2,1,0:T(8,128)(2,1)S(1)} %get-tuple-element.16), channel_id=1, source_target_pairs={{0,30},{2,0},{4,2},{6,4},{8,6},{10,8},{12,10},{14,12},{16,14},{18,... | collective-permute-start | bytes 884744 | tf_op jit(solution)/shard_map/ppermute | solution.py:28
  8.4 1.4 %reduce-window.6 = s32[16,5,128]{2,0,1:T(8,128)S(1)} reduce-window(s32[16,5,128]{2,0,1:T(8,128)S(1)} %copy_bitcast_fusion, s32[]{:T(128)} %constant.21.clone.1), window={size=1x1x128 pad=0_0x0_0x127_0}, to_apply=%region_0.0 | reduce-window | flops 1300480 | bytes 81924 | tf_op jit(solution)/shard_map/reduce-window
  9.8 0.2 slice_reduce_fusion
  10.1 0.1 bitcast_bitcast_fusion
  10.2 6.5 %collective-permute-done = bf16[24,12,512]{2,1,0:T(8,128)(2,1)S(1)} collective-permute-done((bf16[24,12,512]{2,1,0:T(8,128)(2,1)S(1)}, bf16[24,12,512]{2,1,0:T(8,128)(2,1)S(1)}, u32[]{:S(2)}, u32[]{:S(2)}) %collective-permute-start) | collective-permute-done | bytes 294944 | tf_op jit(solution)/shard_map/ppermute | solution.py:28
  16.7 0.2 fusion.2
  16.9 0.1 collective-permute-start.1
  16.9 0.1 pad_add_fusion.first_ref
  17.0 1.5 %collective-permute-done.1 = bf16[12,24,512]{2,1,0:T(8,128)(2,1)S(1)} collective-permute-done((bf16[12,24,512]{2,1,0:T(8,128)(2,1)S(1)}, bf16[12,24,512]{2,1,0:T(8,128)(2,1)S(1)}, u32[]{:S(2)}, u32[]{:S(2)}) %collective-permute-start.1) | collective-permute-done | bytes 294944 | tf_op jit(solution)/shard_map/ppermute | solution.py:28
  18.5 0.1 pad_maximum_fusion
  18.6 12.2 %attention.1 = (bf16[576,512]{1,0:T(8,128)(2,1)S(1)}, bf16[896,512]{1,0:T(8,128)(2,1)}) custom-call(s32[2]{0:T(128)S(1)} %pad_add_fusion.first_ref, f32[16]{0:T(128)S(1)} %copy-done.4, bf16[576,512]{1,0:T(8,128)(2,1)S(1)} %bitcast.35, bf16[512,1536]{1,0:T(8,128)(2,1)S(1)} %copy-done, bf16[512,512]{1,0:T(8,128)(2,1)S(1)} %copy-done.1, f32[1,512]{1,0:T(1,128)S(1)} %bitcast.38, ...), custom_call_target="tpu_custom_call" | custom-call | tf_op jit(solution)/shard_map/attention/pallas_call | solution.py:218
  30.8 0.0 copy-start.8
  30.8 7.6 %all-to-all-start = ((bf16[16,56,512]{2,1,0:T(8,128)(2,1)}), bf16[16,56,512]{2,1,0:T(8,128)(2,1)S(1)}, u32[]{:S(2)}, u32[]{:S(2)}) async-start(bf16[16,56,512]{2,1,0:T(8,128)(2,1)} %bitcast.39), calls=%async_computation | async-start | bytes 1835008 | tf_op jit(solution)/shard_map/all_to_all | solution.py:365
  38.4 0.1 collective-permute-start.2
  38.5 0.5 collective-permute-start.3
  39.0 2.1 %collective-permute-done.2.refs_1_ = bf16[512,1024]{1,0:T(8,128)(2,1)S(1)} collective-permute-done((bf16[512,1024]{1,0:T(8,128)(2,1)S(1)}, bf16[512,1024]{1,0:T(8,128)(2,1)S(1)}, u32[]{:S(2)}, u32[]{:S(2)}) %collective-permute-start.2) | collective-permute-done | bytes 1048608 | tf_op jit(solution)/shard_map/ppermute | solution.py:28
  41.1 1.0 %copy-done.9 = bf16[512,1024]{1,0:T(8,128)(2,1)} copy-done((bf16[512,1024]{1,0:T(8,128)(2,1)}, bf16[512,1024]{1,0:T(8,128)(2,1)S(1)}, u32[]{:S(2)}) %copy-start.9) | copy-done | bytes 1048600
  42.1 0.7 collective-permute-done.3.refs_3_
  42.8 17.9 %all-to-all-done = bf16[16,56,512]{2,1,0:T(8,128)(2,1)S(1)} async-done(((bf16[16,56,512]{2,1,0:T(8,128)(2,1)}), bf16[16,56,512]{2,1,0:T(8,128)(2,1)S(1)}, u32[]{:S(2)}, u32[]{:S(2)}) %all-to-all-start) | async-done | bytes 917536 | tf_op jit(solution)/shard_map/all_to_all | solution.py:365
  60.7 6.8 %shard_map.109 = bf16[896,512]{1,0:T(8,128)(2,1)} custom-call(bf16[896,512]{1,0:T(8,128)(2,1)S(1)} %bitcast.36, bf16[512,1024]{1,0:T(8,128)(2,1)} %bitcast.43, bf16[512,1024]{1,0:T(8,128)(2,1)} %copy-done.9, bf16[1024,512]{1,0:T(8,128)(2,1)} %bitcast.46, bf16[1024,512]{1,0:T(8,128)(2,1)} %collective-permute-done.3.refs_3_), custom_call_target="tpu_custom_call" | custom-call | flops 3758096384 | bytes 4194304 | tf_op jit(solution)/shard_map/pallas_call | solution.py:369
  67.5 5.5 %all-to-all-start.1 = ((bf16[16,56,512]{2,1,0:T(8,128)(2,1)}), bf16[16,56,512]{2,1,0:T(8,128)(2,1)S(1)}, u32[]{:S(2)}, u32[]{:S(2)}) async-start(bf16[16,56,512]{2,1,0:T(8,128)(2,1)} %bitcast.40), calls=%async_computation.1 | async-start | bytes 1835008 | tf_op jit(solution)/shard_map/all_to_all | solution.py:365
  73.0 0.2 copy.19
  73.2 0.1 copy.20.router_ref
  73.3 0.2 copy.17.ids_ref
  73.5 0.2 fusion.1.target_ref
  73.7 0.5 gate.1
  74.1 19.7 %all-to-all-done.1 = bf16[16,56,512]{2,1,0:T(8,128)(2,1)S(1)} async-done(((bf16[16,56,512]{2,1,0:T(8,128)(2,1)}), bf16[16,56,512]{2,1,0:T(8,128)(2,1)S(1)}, u32[]{:S(2)}, u32[]{:S(2)}) %all-to-all-start.1) | async-done | bytes 917536 | tf_op jit(solution)/shard_map/all_to_all | solution.py:365
  93.8 1.9 %combine.1 = bf16[576,512]{1,0:T(8,128)(2,1)} custom-call(bf16[576,512]{1,0:T(8,128)(2,1)S(1)} %get-tuple-element.9.x1_ref, bf16[576,896]{1,0:T(8,128)(2,1)S(1)} %get-tuple-element.10.pick_ref, f32[576,1]{1,0:T(8,128)S(1)} %get-tuple-element.11.scaled_ref, f32[1,512]{1,0:T(1,128)S(1)} %bitcast.37, bf16[896,512]{1,0:T(8,128)(2,1)S(1)} %bitcast.34), custom_call_target="tpu_custom_call" | custom-call | tf_op jit(solution)/shard_map/combine/pallas_call | solution.py:405
  (23 shorter events, 0.1 us)
Async XLA Ops:
  0.0 8.3 %copy-start.5 = (s32[1,1,576,1]{2,3,1,0:T(1,128)S(1)}, s32[1,1,576,1]{2,3,1,0:T(1,128)}, u32[]{:S(2)}) copy-start(s32[1,1,576,1]{2,3,1,0:T(1,128)} %param.20) | copy-start | bytes 6916
  0.0 8.3 %copy-start.6 = (s32[1,1,576]{2,1,0:T(1,128)S(1)}, s32[1,1,576]{2,1,0:T(1,128)}, u32[]{:S(2)}) copy-start(s32[1,1,576]{2,1,0:T(1,128)} %param.21) | copy-start | bytes 6916
  1.3 17.3 %copy-start = (bf16[512,1536]{1,0:T(8,128)(2,1)S(1)}, bf16[512,1536]{1,0:T(8,128)(2,1)}, u32[]{:S(2)}) copy-start(bf16[512,1536]{1,0:T(8,128)(2,1)} %wqkv_ref.1) | copy-start | bytes 4718596
  1.3 17.3 %copy-start.1 = (bf16[512,512]{1,0:T(8,128)(2,1)S(1)}, bf16[512,512]{1,0:T(8,128)(2,1)}, u32[]{:S(2)}) copy-start(bf16[512,512]{1,0:T(8,128)(2,1)} %wproj_ref.1) | copy-start | bytes 1572868
  1.3 17.3 %copy-start.3 = (f32[512]{0:T(512)S(1)}, f32[512]{0:T(512)}, u32[]{:S(2)}) copy-start(f32[512]{0:T(512)} %param.15) | copy-start | bytes 6148
  1.3 17.3 %copy-start.4 = (f32[16]{0:T(128)S(1)}, f32[16]{0:T(128)}, u32[]{:S(2)}) copy-start(f32[16]{0:T(128)} %scale_ref.1) | copy-start | bytes 196
  1.3 15.4 %collective-permute-start = (bf16[24,12,512]{2,1,0:T(8,128)(2,1)S(1)}, bf16[24,12,512]{2,1,0:T(8,128)(2,1)S(1)}, u32[]{:S(2)}, u32[]{:S(2)}) collective-permute-start(bf16[24,12,512]{2,1,0:T(8,128)(2,1)S(1)} %get-tuple-element.16), channel_id=1, source_target_pairs={{0,30},{2,0},{4,2},{6,4},{8,6},{10,8},{12,10},{14,12},{16,14},{18,... | collective-permute-start | bytes 884744 | tf_op jit(solution)/shard_map/ppermute | solution.py:28
  16.9 1.6 %collective-permute-start.1 = (bf16[12,24,512]{2,1,0:T(8,128)(2,1)S(1)}, bf16[12,24,512]{2,1,0:T(8,128)(2,1)S(1)}, u32[]{:S(2)}, u32[]{:S(2)}) collective-permute-start(bf16[12,24,512]{2,1,0:T(8,128)(2,1)S(1)} %get-tuple-element.14), channel_id=1, source_target_pairs={{0,1},{1,0},{2,3},{3,2},{4,5},{5,4},{6,7},{7,6},{8,9},{9,8},{10,11... | collective-permute-start | bytes 884744 | tf_op jit(solution)/shard_map/ppermute | solution.py:28
  30.8 7.6 %copy-start.8 = (bf16[1,512,1024]{2,1,0:T(8,128)(2,1)S(1)}, bf16[1,512,1024]{2,1,0:T(8,128)(2,1)}, u32[]{:S(2)}) copy-start(bf16[1,512,1024]{2,1,0:T(8,128)(2,1)} %param.17) | copy-start | bytes 3145732
  30.8 29.9 %all-to-all-start = ((bf16[16,56,512]{2,1,0:T(8,128)(2,1)}), bf16[16,56,512]{2,1,0:T(8,128)(2,1)S(1)}, u32[]{:S(2)}, u32[]{:S(2)}) async-start(bf16[16,56,512]{2,1,0:T(8,128)(2,1)} %bitcast.39), calls=%async_computation | async-start | bytes 1835008 | tf_op jit(solution)/shard_map/all_to_all | solution.py:365
  38.4 2.7 %collective-permute-start.2 = (bf16[512,1024]{1,0:T(8,128)(2,1)S(1)}, bf16[512,1024]{1,0:T(8,128)(2,1)S(1)}, u32[]{:S(2)}, u32[]{:S(2)}) collective-permute-start(bf16[512,1024]{1,0:T(8,128)(2,1)S(1)} %bitcast.44), channel_id=1, source_target_pairs={{0,1},{1,0},{2,3},{3,2},{4,5},{5,4},{6,7},{7,6},{8,9},{9,8},{10,11... | collective-permute-start | bytes 3145736 | tf_op jit(solution)/shard_map/ppermute | solution.py:28
  38.5 4.3 %collective-permute-start.3 = (bf16[1024,512]{1,0:T(8,128)(2,1)}, bf16[1024,512]{1,0:T(8,128)(2,1)}, u32[]{:S(2)}, u32[]{:S(2)}) collective-permute-start(bf16[1024,512]{1,0:T(8,128)(2,1)} %bitcast.45), channel_id=1, source_target_pairs={{0,1},{1,0},{2,3},{3,2},{4,5},{5,4},{6,7},{7,6},{8,9},{9,8},{10,11... | collective-permute-start | bytes 3145736 | tf_op jit(solution)/shard_map/ppermute | solution.py:28
  41.1 1.0 %copy-start.9 = (bf16[512,1024]{1,0:T(8,128)(2,1)}, bf16[512,1024]{1,0:T(8,128)(2,1)S(1)}, u32[]{:S(2)}) copy-start(bf16[512,1024]{1,0:T(8,128)(2,1)S(1)} %collective-permute-done.2.refs_1_) | copy-start | bytes 3145732
  67.4 5.8 %copy-start.7 = (bf16[512,16]{0,1:T(8,128)(2,1)S(1)}, bf16[512,16]{0,1:T(8,128)(2,1)}, u32[]{:S(2)}) copy-start(bf16[512,16]{0,1:T(8,128)(2,1)} %param.16) | copy-start | bytes 49156
  67.5 26.4 %all-to-all-start.1 = ((bf16[16,56,512]{2,1,0:T(8,128)(2,1)}), bf16[16,56,512]{2,1,0:T(8,128)(2,1)S(1)}, u32[]{:S(2)}, u32[]{:S(2)}) async-start(bf16[16,56,512]{2,1,0:T(8,128)(2,1)} %bitcast.40), calls=%async_computation.1 | async-start | bytes 1835008 | tf_op jit(solution)/shard_map/all_to_all | solution.py:365
  73.0 20.9 %copy-start.2 = (f32[512]{0:T(512)S(1)}, f32[512]{0:T(512)}, u32[]{:S(2)}) copy-start(f32[512]{0:T(512)} %param.19) | copy-start | bytes 6148
where the time goes:
time: 96 us; the launch traced here: 95.7 us
  waiting for transfers between devices  48.3 us (50%)
  Pallas kernels  21.2 us (22%)
  starting transfers between devices  20.8 us (22%)
  local copies, waits for them, and re-layouts  3.01 us (3%)
  other arithmetic  2.07 us (2%)
    all_to_all x2, waiting for transfers between devices, exchange(): lax.all_to_all(value, 'wide', split_axis=0, concat_axis=0, tiled=True)  37.6 us
    all_to_all x2, starting transfers between devices, exchange(): lax.all_to_all(value, 'wide', split_axis=0, concat_axis=0, tiled=True)  13.1 us
    pallas_call x1, Pallas kernels, call_attn(): pl.pallas_call(functools.partial(attn_kernel, grid_rc, head_dim, edge, ro...  12.2 us
    ppermute x4, waiting for transfers between devices, shifted(): lax.ppermute(value, axis, [(i, (i + by) % peers) for i in range(peers)])  10.8 us
    ppermute x4, starting transfers between devices, shifted(): lax.ppermute(value, axis, [(i, (i + by) % peers) for i in range(peers)])  7.65 us
    pallas_call x1, Pallas kernels, run_experts(): pl.pallas_call(functools.partial(expert_kernel, tall, rows // 2 if rows >...  6.77 us
  transfers between devices with their start and end apart: 6, of which 6 were waited for; matrix products, arithmetic and copies ran while one was open for 3% of the time, Pallas kernels for 0%

commit v1 on v0

--- a/solution.py
+++ b/solution.py
@@ -238,30 +238,36 @@
     )(first, head_scale, rolled, qkv, proj, gain, target)
 
 
-def expert_kernel(parts, row_block, x_ref, *refs):
+def expert_kernel(parts, pieces, row_block, x_ref, *refs):
     w_in, w_out, y_ref = refs[:parts], refs[parts : 2 * parts], refs[2 * parts]
-    in_s, out_s, acc_s, sem = refs[2 * parts + 1 :]
-    rows = x_ref.shape[0]
-    copies = []
+    in_s, out_s, sem = refs[2 * parts + 1 :]
+    feature, hidden = w_in[0].shape
+    deep, wide = feature // pieces, hidden // pieces
+    ins, outs = [], []
     for n in range(parts):
-        copies.append(pltpu.make_async_copy(w_in[n], in_s.at[n], sem.at[2 * n]))
-        copies.append(pltpu.make_async_copy(w_out[n], out_s.at[n], sem.at[2 * n + 1]))
-    for copy in copies:
+        for i in range(pieces):
+            k = 2 * (n * pieces + i)
+            rows = pl.ds(i * deep, deep)
+            if n:
+                ins.append(pltpu.make_async_copy(w_in[n].at[rows], in_s.at[rows, pl.ds((n - 1) * hidden, hidden)], sem.at[k]))
+            outs.append(
+                pltpu.make_async_copy(
+                    w_out[n].at[pl.ds(i * wide, wide)], out_s.at[pl.ds(n * hidden + i * wide, wide)], sem.at[k + 1]
+                )
+            )
+    for copy in ins + outs:
         copy.start()
-    for n in range(parts):
-        copies[2 * n].wait()
-        copies[2 * n + 1].wait()
-        for i in range(rows // row_block):
-            part = slice(i * row_block, (i + 1) * row_block)
-            h = dot(x_ref[part, :], in_s[n])
-            h = (0.5 * h * (1.0 + lax.erf(h * 0.7071067811865476))).astype(jnp.bfloat16)
-            y = dot(h, out_s[n])
-            if n:
-                y = acc_s[part, :] + y
-            if n < parts - 1:
-                acc_s[part, :] = y
-            else:
-                y_ref[part, :] = y.astype(jnp.bfloat16)
+
+    def gelu(h):
+        return (0.5 * h * (1.0 + lax.erf(h * 0.7071067811865476))).astype(jnp.bfloat16)
+
+    blocks = [slice(at, at + row_block) for at in range(0, x_ref.shape[0], row_block)]
+    own = [gelu(dot(x_ref[block, :], w_in[0][...])) for block in blocks]
+    for copy in ins + outs:
+        copy.wait()
+    for block, h in zip(blocks, own):
+        h = jnp.concatenate([h, gelu(dot(x_ref[block, :], in_s[...]))], axis=1)
+        y_ref[block, :] = dot(h, out_s[...]).astype(jnp.bfloat16)
 
 
 def gate_kernel(x1_ref, router_ref, target_ref, ids_ref, pick_ref, scaled_ref):
@@ -357,7 +363,7 @@
         sizes=tuple(experts * part for part in parts),
     )
     hidden = w_in[0].shape[1]
-    weights = [pltpu.with_memory_space_constraint(w, pltpu.HBM) for w in w_in + w_out]
+    weights = w_in[:1] + [pltpu.with_memory_space_constraint(w, pltpu.HBM) for w in w_in[1:] + w_out]
 
     def exchange(value):
         rows = value.shape[0]
@@ -367,15 +373,14 @@
     def run_experts(value):
         rows = value.shape[0]
         return pl.pallas_call(
-            functools.partial(expert_kernel, tall, rows // 2 if rows > 512 else rows),
+            functools.partial(expert_kernel, tall, max(1, 4 // tall), rows // 2 if rows > 512 else rows),
             out_shape=pltpu.HBM((rows, feature), jnp.bfloat16),
-            in_specs=[VM] + [HB] * (2 * tall),
+            in_specs=[VM] * 2 + [HB] * (2 * tall - 1),
             out_specs=VM,
             scratch_shapes=[
-                pltpu.VMEM((tall, feature, hidden), jnp.bfloat16),
-                pltpu.VMEM((tall, hidden, feature), jnp.bfloat16),
-                pltpu.VMEM((rows, feature), jnp.float32),
-                pltpu.SemaphoreType.DMA((2 * tall,)),
+                pltpu.VMEM((feature, (tall - 1) * hidden), jnp.bfloat16),
+                pltpu.VMEM((tall * hidden, feature), jnp.bfloat16),
+                pltpu.SemaphoreType.DMA((2 * tall * max(1, 4 // tall),)),
             ],
             compiler_params=params(32),
             cost_estimate=pl.CostEstimate(

time: 96 us -> 95.3 us (level)
  no operation moved by 1% of the time
where the time goes in v1:
time: 95.3 us; the launch traced here: 95 us
  waiting for transfers between devices  48.3 us (51%)
  starting transfers between devices  20.8 us (22%)
  Pallas kernels  20.5 us (22%)
  local copies, waits for them, and re-layouts  3.01 us (3%)
  other arithmetic  2.07 us (2%)
    all_to_all x2, waiting for transfers between devices, exchange(): lax.all_to_all(value, 'wide', split_axis=0, concat_axis=0, tiled=True)  37.6 us
    all_to_all x2, starting transfers between devices, exchange(): lax.all_to_all(value, 'wide', split_axis=0, concat_axis=0, tiled=True)  13.1 us
    pallas_call x1, Pallas kernels, call_attn(): pl.pallas_call(functools.partial(attn_kernel, grid_rc, head_dim, edge, ro...  12.2 us
    ppermute x4, waiting for transfers between devices, shifted(): lax.ppermute(value, axis, [(i, (i + by) % peers) for i in range(peers)])  10.8 us
    ppermute x4, starting transfers between devices, shifted(): lax.ppermute(value, axis, [(i, (i + by) % peers) for i in range(peers)])  7.65 us
    pallas_call x1, Pallas kernels, run_experts(): pl.pallas_call(functools.partial(expert_kernel, tall, max(1, 4 // tall),...  6.06 us
  transfers between devices with their start and end apart: 6, of which 6 were waited for; matrix products, arithmetic and copies ran while one was open for 3% of the time, Pallas kernels for 0%

profile of v1, /device:TPU:0, one launch (start us, length us, event | category | flops | bytes accessed | tf_op | source)
XLA Modules:
  0.0 95.0 jit_solution(1719202457299450224)
XLA Ops:
  0.0 1.3 %fusion.7 = (bf16[24,12,512]{2,1,0:T(8,128)(2,1)S(1)}, bf16[24,12,512]{2,1,0:T(8,128)(2,1)S(1)}) fusion(bf16[24,24,512]{2,1,0:T(8,128)(2,1)} %param.11), kind=kLoop, calls=%fused_computation.27 | loop fusion | bytes 1179648 | tf_op jit(solution)/shard_map/slice | solution.py:324
  1.3 0.0 copy-start
  1.3 0.0 copy-start.1
  1.3 7.0 %collective-permute-start = (bf16[24,12,512]{2,1,0:T(8,128)(2,1)S(1)}, bf16[24,12,512]{2,1,0:T(8,128)(2,1)S(1)}, u32[]{:S(2)}, u32[]{:S(2)}) collective-permute-start(bf16[24,12,512]{2,1,0:T(8,128)(2,1)S(1)} %get-tuple-element.16), channel_id=1, source_target_pairs={{0,30},{2,0},{4,2},{6,4},{8,6},{10,8},{12,10},{14,12},{16,14},{18,... | collective-permute-start | bytes 884744 | tf_op jit(solution)/shard_map/ppermute | solution.py:28
  8.4 1.4 %reduce-window.6 = s32[16,5,128]{2,0,1:T(8,128)S(1)} reduce-window(s32[16,5,128]{2,0,1:T(8,128)S(1)} %copy_bitcast_fusion, s32[]{:T(128)} %constant.21.clone.1), window={size=1x1x128 pad=0_0x0_0x127_0}, to_apply=%region_0.0 | reduce-window | flops 1300480 | bytes 81924 | tf_op jit(solution)/shard_map/reduce-window
  9.8 0.2 slice_reduce_fusion
  10.1 0.1 bitcast_bitcast_fusion
  10.2 6.5 %collective-permute-done = bf16[24,12,512]{2,1,0:T(8,128)(2,1)S(1)} collective-permute-done((bf16[24,12,512]{2,1,0:T(8,128)(2,1)S(1)}, bf16[24,12,512]{2,1,0:T(8,128)(2,1)S(1)}, u32[]{:S(2)}, u32[]{:S(2)}) %collective-permute-start) | collective-permute-done | bytes 294944 | tf_op jit(solution)/shard_map/ppermute | solution.py:28
  16.7 0.2 fusion.2
  16.9 0.1 collective-permute-start.1
  16.9 0.1 pad_add_fusion.first_ref
  17.0 1.5 %collective-permute-done.1 = bf16[12,24,512]{2,1,0:T(8,128)(2,1)S(1)} collective-permute-done((bf16[12,24,512]{2,1,0:T(8,128)(2,1)S(1)}, bf16[12,24,512]{2,1,0:T(8,128)(2,1)S(1)}, u32[]{:S(2)}, u32[]{:S(2)}) %collective-permute-start.1) | collective-permute-done | bytes 294944 | tf_op jit(solution)/shard_map/ppermute | solution.py:28
  18.5 0.1 pad_maximum_fusion
  18.6 12.2 %attention.1 = (bf16[576,512]{1,0:T(8,128)(2,1)S(1)}, bf16[896,512]{1,0:T(8,128)(2,1)}) custom-call(s32[2]{0:T(128)S(1)} %pad_add_fusion.first_ref, f32[16]{0:T(128)S(1)} %copy-done.4, bf16[576,512]{1,0:T(8,128)(2,1)S(1)} %bitcast.35, bf16[512,1536]{1,0:T(8,128)(2,1)S(1)} %copy-done, bf16[512,512]{1,0:T(8,128)(2,1)S(1)} %copy-done.1, f32[1,512]{1,0:T(1,128)S(1)} %bitcast.38, ...), custom_call_target="tpu_custom_call" | custom-call | tf_op jit(solution)/shard_map/attention/pallas_call | solution.py:218
  30.8 0.0 copy-start.5
  30.8 7.6 %all-to-all-start = ((bf16[16,56,512]{2,1,0:T(8,128)(2,1)}), bf16[16,56,512]{2,1,0:T(8,128)(2,1)S(1)}, u32[]{:S(2)}, u32[]{:S(2)}) async-start(bf16[16,56,512]{2,1,0:T(8,128)(2,1)} %bitcast.41), calls=%async_computation | async-start | bytes 1835008 | tf_op jit(solution)/shard_map/all_to_all | solution.py:371
  38.4 0.1 collective-permute-start.2
  38.5 0.5 collective-permute-start.3
  39.0 2.1 %collective-permute-done.2.refs_1_ = bf16[512,1024]{1,0:T(8,128)(2,1)S(1)} collective-permute-done((bf16[512,1024]{1,0:T(8,128)(2,1)S(1)}, bf16[512,1024]{1,0:T(8,128)(2,1)S(1)}, u32[]{:S(2)}, u32[]{:S(2)}) %collective-permute-start.2) | collective-permute-done | bytes 1048608 | tf_op jit(solution)/shard_map/ppermute | solution.py:28
  41.1 1.0 %copy-done.9 = bf16[512,1024]{1,0:T(8,128)(2,1)} copy-done((bf16[512,1024]{1,0:T(8,128)(2,1)}, bf16[512,1024]{1,0:T(8,128)(2,1)S(1)}, u32[]{:S(2)}) %copy-start.9) | copy-done | bytes 1048600
  42.1 0.7 collective-permute-done.3.refs_3_
  42.8 17.9 %all-to-all-done = bf16[16,56,512]{2,1,0:T(8,128)(2,1)S(1)} async-done(((bf16[16,56,512]{2,1,0:T(8,128)(2,1)}), bf16[16,56,512]{2,1,0:T(8,128)(2,1)S(1)}, u32[]{:S(2)}, u32[]{:S(2)}) %all-to-all-start) | async-done | bytes 917536 | tf_op jit(solution)/shard_map/all_to_all | solution.py:371
  60.7 6.1 %shard_map.109 = bf16[896,512]{1,0:T(8,128)(2,1)} custom-call(bf16[896,512]{1,0:T(8,128)(2,1)S(1)} %bitcast.36, bf16[512,1024]{1,0:T(8,128)(2,1)S(1)} %bitcast.40, bf16[512,1024]{1,0:T(8,128)(2,1)} %copy-done.9, bf16[1024,512]{1,0:T(8,128)(2,1)} %bitcast.46, bf16[1024,512]{1,0:T(8,128)(2,1)} %collective-permute-done.3.refs_3_), custom_call_target="tpu_custom_call" | custom-call | flops 3758096384 | bytes 4194304 | tf_op jit(solution)/shard_map/pallas_call | solution.py:375
  66.8 5.5 %all-to-all-start.1 = ((bf16[16,56,512]{2,1,0:T(8,128)(2,1)}), bf16[16,56,512]{2,1,0:T(8,128)(2,1)S(1)}, u32[]{:S(2)}, u32[]{:S(2)}) async-start(bf16[16,56,512]{2,1,0:T(8,128)(2,1)} %bitcast.42), calls=%async_computation.1 | async-start | bytes 1835008 | tf_op jit(solution)/shard_map/all_to_all | solution.py:371
  72.3 0.0 copy-start.2
  72.3 0.2 copy.19
  72.5 0.1 copy.20.router_ref
  72.6 0.2 copy.17.ids_ref
  72.8 0.2 fusion.1.target_ref
  73.0 0.5 gate.1
  73.4 19.7 %all-to-all-done.1 = bf16[16,56,512]{2,1,0:T(8,128)(2,1)S(1)} async-done(((bf16[16,56,512]{2,1,0:T(8,128)(2,1)}), bf16[16,56,512]{2,1,0:T(8,128)(2,1)S(1)}, u32[]{:S(2)}, u32[]{:S(2)}) %all-to-all-start.1) | async-done | bytes 917536 | tf_op jit(solution)/shard_map/all_to_all | solution.py:371
  93.1 1.9 %combine.1 = bf16[576,512]{1,0:T(8,128)(2,1)} custom-call(bf16[576,512]{1,0:T(8,128)(2,1)S(1)} %get-tuple-element.9.x1_ref, bf16[576,896]{1,0:T(8,128)(2,1)S(1)} %get-tuple-element.10.pick_ref, f32[576,1]{1,0:T(8,128)S(1)} %get-tuple-element.11.scaled_ref, f32[1,512]{1,0:T(1,128)S(1)} %bitcast.37, bf16[896,512]{1,0:T(8,128)(2,1)S(1)} %bitcast.34), custom_call_target="tpu_custom_call" | custom-call | tf_op jit(solution)/shard_map/combine/pallas_call | solution.py:410
  (23 shorter events, 0.1 us)
Async XLA Ops:
  0.0 8.3 %copy-start.6 = (s32[1,1,576,1]{2,3,1,0:T(1,128)S(1)}, s32[1,1,576,1]{2,3,1,0:T(1,128)}, u32[]{:S(2)}) copy-start(s32[1,1,576,1]{2,3,1,0:T(1,128)} %param.20) | copy-start | bytes 6916
  0.0 8.3 %copy-start.7 = (s32[1,1,576]{2,1,0:T(1,128)S(1)}, s32[1,1,576]{2,1,0:T(1,128)}, u32[]{:S(2)}) copy-start(s32[1,1,576]{2,1,0:T(1,128)} %param.21) | copy-start | bytes 6916
  1.3 17.3 %copy-start = (bf16[512,1536]{1,0:T(8,128)(2,1)S(1)}, bf16[512,1536]{1,0:T(8,128)(2,1)}, u32[]{:S(2)}) copy-start(bf16[512,1536]{1,0:T(8,128)(2,1)} %wqkv_ref.1) | copy-start | bytes 4718596
  1.3 17.3 %copy-start.1 = (bf16[512,512]{1,0:T(8,128)(2,1)S(1)}, bf16[512,512]{1,0:T(8,128)(2,1)}, u32[]{:S(2)}) copy-start(bf16[512,512]{1,0:T(8,128)(2,1)} %wproj_ref.1) | copy-start | bytes 1572868
  1.3 17.3 %copy-start.3 = (f32[512]{0:T(512)S(1)}, f32[512]{0:T(512)}, u32[]{:S(2)}) copy-start(f32[512]{0:T(512)} %param.15) | copy-start | bytes 6148
  1.3 17.3 %copy-start.4 = (f32[16]{0:T(128)S(1)}, f32[16]{0:T(128)}, u32[]{:S(2)}) copy-start(f32[16]{0:T(128)} %scale_ref.1) | copy-start | bytes 196
  1.3 15.4 %collective-permute-start = (bf16[24,12,512]{2,1,0:T(8,128)(2,1)S(1)}, bf16[24,12,512]{2,1,0:T(8,128)(2,1)S(1)}, u32[]{:S(2)}, u32[]{:S(2)}) collective-permute-start(bf16[24,12,512]{2,1,0:T(8,128)(2,1)S(1)} %get-tuple-element.16), channel_id=1, source_target_pairs={{0,30},{2,0},{4,2},{6,4},{8,6},{10,8},{12,10},{14,12},{16,14},{18,... | collective-permute-start | bytes 884744 | tf_op jit(solution)/shard_map/ppermute | solution.py:28
  16.9 1.6 %collective-permute-start.1 = (bf16[12,24,512]{2,1,0:T(8,128)(2,1)S(1)}, bf16[12,24,512]{2,1,0:T(8,128)(2,1)S(1)}, u32[]{:S(2)}, u32[]{:S(2)}) collective-permute-start(bf16[12,24,512]{2,1,0:T(8,128)(2,1)S(1)} %get-tuple-element.14), channel_id=1, source_target_pairs={{0,1},{1,0},{2,3},{3,2},{4,5},{5,4},{6,7},{7,6},{8,9},{9,8},{10,11... | collective-permute-start | bytes 884744 | tf_op jit(solution)/shard_map/ppermute | solution.py:28
  30.8 7.6 %copy-start.5 = (bf16[1,512,1024]{2,1,0:T(8,128)(2,1)S(1)}, bf16[1,512,1024]{2,1,0:T(8,128)(2,1)}, u32[]{:S(2)}) copy-start(bf16[1,512,1024]{2,1,0:T(8,128)(2,1)} %param.17) | copy-start | bytes 3145732
  30.8 29.9 %all-to-all-start = ((bf16[16,56,512]{2,1,0:T(8,128)(2,1)}), bf16[16,56,512]{2,1,0:T(8,128)(2,1)S(1)}, u32[]{:S(2)}, u32[]{:S(2)}) async-start(bf16[16,56,512]{2,1,0:T(8,128)(2,1)} %bitcast.41), calls=%async_computation | async-start | bytes 1835008 | tf_op jit(solution)/shard_map/all_to_all | solution.py:371
  38.4 2.7 %collective-permute-start.2 = (bf16[512,1024]{1,0:T(8,128)(2,1)S(1)}, bf16[512,1024]{1,0:T(8,128)(2,1)S(1)}, u32[]{:S(2)}, u32[]{:S(2)}) collective-permute-start(bf16[512,1024]{1,0:T(8,128)(2,1)S(1)} %bitcast.39), channel_id=1, source_target_pairs={{0,1},{1,0},{2,3},{3,2},{4,5},{5,4},{6,7},{7,6},{8,9},{9,8},{10,11... | collective-permute-start | bytes 3145736 | tf_op jit(solution)/shard_map/ppermute | solution.py:28
  38.5 4.3 %collective-permute-start.3 = (bf16[1024,512]{1,0:T(8,128)(2,1)}, bf16[1024,512]{1,0:T(8,128)(2,1)}, u32[]{:S(2)}, u32[]{:S(2)}) collective-permute-start(bf16[1024,512]{1,0:T(8,128)(2,1)} %bitcast.45), channel_id=1, source_target_pairs={{0,1},{1,0},{2,3},{3,2},{4,5},{5,4},{6,7},{7,6},{8,9},{9,8},{10,11... | collective-permute-start | bytes 3145736 | tf_op jit(solution)/shard_map/ppermute | solution.py:28
  41.1 1.0 %copy-start.9 = (bf16[512,1024]{1,0:T(8,128)(2,1)}, bf16[512,1024]{1,0:T(8,128)(2,1)S(1)}, u32[]{:S(2)}) copy-start(bf16[512,1024]{1,0:T(8,128)(2,1)S(1)} %collective-permute-done.2.refs_1_) | copy-start | bytes 3145732
  66.7 5.8 %copy-start.8 = (bf16[512,16]{0,1:T(8,128)(2,1)S(1)}, bf16[512,16]{0,1:T(8,128)(2,1)}, u32[]{:S(2)}) copy-start(bf16[512,16]{0,1:T(8,128)(2,1)} %param.16) | copy-start | bytes 49156
  66.8 26.4 %all-to-all-start.1 = ((bf16[16,56,512]{2,1,0:T(8,128)(2,1)}), bf16[16,56,512]{2,1,0:T(8,128)(2,1)S(1)}, u32[]{:S(2)}, u32[]{:S(2)}) async-start(bf16[16,56,512]{2,1,0:T(8,128)(2,1)} %bitcast.42), calls=%async_computation.1 | async-start | bytes 1835008 | tf_op jit(solution)/shard_map/all_to_all | solution.py:371
  72.3 20.9 %copy-start.2 = (f32[512]{0:T(512)S(1)}, f32[512]{0:T(512)}, u32[]{:S(2)}) copy-start(f32[512]{0:T(512)} %param.19) | copy-start | bytes 6148
